TPU v7x, 32 devices: a whole 2x2x4 slice. The times are simulated.
32 devices in a mesh: freq: 8 (over y, x, core), base: 4 (over z).
Axes of the slice: x: 2, y: 2, z: 4, core: 2. Of those that a mesh axis runs over, the one named last changes fastest.
Arguments:
- visibility: float32 [2, 16, 2048], P(None, 'freq', 'base'), may hold values from -6 to 6
- tile_of: int32 [16, 2048, 1], P('freq', 'base'), may hold values from 0 to 3; in each aligned block of 512 rows (0 to 511, 512 to 1023, ..., all dimensions but the last counted through in order) at most 256 rows name the same one
- u_within: int32 [16, 2048], P('freq', 'base'), may hold values from 0 to 255
- v_cell: int32 [16, 2048], P('freq', 'base'), may hold values from 0 to 1016
- kernel_index: int32 [2, 16, 2048], P(None, 'freq', 'base'), may hold values from 0 to 127
- kernel: float32 [128, 8], replicated, may hold values from 0.1 to 1
- live_count: int32 [16, 4], P('freq', 'base'), may hold values from 64 to 512, as said below
- bin_map: int32 [1024, 1024], P('base'), may hold values from 0 to 511, as said below
Outputs:
- power_map: float32 [1024, 1024], P('freq', 'base')
- spectrum: float32 [512], replicated
Inputs may be any that keep to these rules, and one draw needn't show every extreme that they name: `tile_of`: among the visibilities of one channel on one device, at most 256 name the same tile, and in some device's visibilities a tile is named by exactly 256. `live_count`: the first device along base holds 512 used slots in every channel; the used slots of a device are its first ones. `bin_map`: every bin number occurs.
All inputs are finite; a program needn't handle non-finite values.
Results may differ from a plain program's by a relative error of at most 0.0003.
Values sent between devices are 32-bit elements; how exact they have to be, the bound alone decides.
No kernel may reach another device: no remote copies, remote signals or barrier semaphores. Data moves between devices by JAX's collectives and lax.ppermute only.
A program may use at most 128 MiB of HBM per device.

v0:
```python
import math

import jax
import jax.numpy as jnp
from jax import lax
from jax.sharding import PartitionSpec as P

G = 1024
NBINS = 512
KW = 8


HIGHEST_PRECISION = lax.Precision.HIGHEST


def passed_along(x, axis, by):
    peers = lax.axis_size(axis)
    pairs = [(i, i + by) for i in range(peers) if 0 <= i + by < peers]
    return lax.ppermute(x, axis, pairs)


def look_up_taps(kernel_index, kernel):
    table_rows = kernel.shape[0]
    onehot = (kernel_index[..., None] == jnp.arange(table_rows, dtype=jnp.int32)).astype(
        jnp.float32
    )
    return jnp.einsum("acno,ot->actn", onehot, kernel, precision=HIGHEST_PRECISION)


def visibility_fields(
    visibility, tile_of, u_within, v_cell, kernel_index, kernel, live_count, tile_rows
):
    slots = u_within.shape[1]
    is_live = jnp.arange(slots, dtype=jnp.int32)[None, :] < live_count
    zeroed = jnp.zeros_like(visibility[0])
    real_part = jnp.where(is_live, visibility[0], zeroed)
    imag_part = jnp.where(is_live, visibility[1], zeroed)
    tile_index = tile_of[:, :, 0]
    u_cell = jnp.minimum(tile_index * tile_rows + u_within, G - KW)
    u_cell = u_cell - tile_index * tile_rows
    taps = look_up_taps(kernel_index, kernel)
    fields = jnp.concatenate(
        [
            real_part[:, None],
            imag_part[:, None],
            u_cell[:, None].astype(jnp.float32),
            v_cell[:, None].astype(jnp.float32),
            taps[0],
            taps[1],
        ],
        axis=1,
    )
    return (fields, is_live, tile_index)


def row_taps(fields, row_start, row_count):
    u_cell = fields[2].astype(jnp.int32)
    offset = row_start + jnp.arange(row_count, dtype=jnp.int32)[None, :] - u_cell[:, None]
    taps = jnp.zeros(offset.shape, jnp.float32)
    for tap_index in range(KW):
        taps = taps + jnp.where(offset == tap_index, fields[4 + tap_index][:, None], 0.0)
    return taps


def column_side(fields):
    v_start = fields[3].astype(jnp.int32)
    offset = jnp.arange(G, dtype=jnp.int32)[None, :] - v_start[:, None]
    taps = jnp.zeros(offset.shape, jnp.float32)
    for tap_index in range(KW):
        taps = taps + jnp.where(offset == tap_index, fields[4 + KW + tap_index][:, None], 0.0)
    return jnp.concatenate([fields[0][:, None] * taps, fields[1][:, None] * taps], axis=1)


def contract_slots(upper, lower):
    return lax.dot_general(upper, lower, (((0,), (0,)), ((), ())), precision=HIGHEST_PRECISION)


def grid_rows(fields, row_start, row_count):
    return contract_slots(row_taps(fields, row_start, row_count), column_side(fields))


def dft_matrix():
    positions = jnp.arange(G, dtype=jnp.int32)
    phase = positions[:, None] * positions[None, :] % G
    angle = phase.astype(jnp.float32) * (2.0 * math.pi / G)
    cosine = jnp.cos(angle)
    sine = jnp.sin(angle)
    return jnp.concatenate(
        [jnp.concatenate([cosine, -sine], axis=1), jnp.concatenate([sine, cosine], axis=1)], axis=0
    )


def row_transform(grid_tile, dft_table, tile_rows, channels_here):
    flat_rows = grid_tile.reshape(tile_rows * channels_here, 2 * G)
    halves = jnp.stack(
        [
            jnp.dot(flat_rows, dft_table[:, :G], precision=HIGHEST_PRECISION),
            jnp.dot(flat_rows, dft_table[:, G:], precision=HIGHEST_PRECISION),
        ]
    )
    return halves.reshape(2, tile_rows, channels_here, G)


def to_columns(columns, tile_rows, channels_here):
    return columns.reshape(2 * G, channels_here * tile_rows)


def histogram(stacked, bins):
    row_total = bins.shape[0]
    block_rows = min(64, row_total)
    block_count = row_total // block_rows
    columns = bins.shape[1]
    value_blocks = stacked.reshape(2, block_count, block_rows * columns).transpose(1, 0, 2)
    bin_blocks = bins.reshape(block_count, block_rows * columns)

    def add_block(running, pieces):
        values, bin_ids = pieces
        onehot = (bin_ids[:, None] == jnp.arange(NBINS, dtype=jnp.int32)[None, :]).astype(
            jnp.float32
        )
        return (running + jnp.dot(values, onehot, precision=HIGHEST_PRECISION), None)

    result, _ = lax.scan(add_block, jnp.zeros((2, NBINS), jnp.float32), (value_blocks, bin_blocks))
    return result


def per_device(visibility, tile_of, u_within, v_cell, kernel_index, kernel, live_count, bin_map):
    base_count = lax.axis_size("base")
    freq_count = lax.axis_size("freq")
    tile_rows = G // base_count
    channels_here = visibility.shape[1]
    slots = visibility.shape[2]
    dft_table = dft_matrix()
    fields, is_live, tile_index = visibility_fields(
        visibility, tile_of, u_within, v_cell, kernel_index, kernel, live_count, tile_rows
    )
    capacity = 2 * slots // base_count
    field_count = fields.shape[1]
    chosen = (
        (tile_index[:, :, None] == jnp.arange(base_count, dtype=jnp.int32)[None, None, :])
        & is_live[:, :, None]
    ).astype(jnp.int32)
    before_count = jnp.sum((jnp.cumsum(chosen, axis=1) - chosen) * chosen, axis=2)
    target = jnp.where(is_live, tile_index * capacity + before_count, base_count * capacity)
    outgoing = []
    for channel in range(channels_here):
        placed = (
            jnp.zeros((base_count * capacity, field_count), jnp.float32)
            .at[target[channel]]
            .set(fields[channel].T, mode="drop")
        )
        outgoing.append(placed.reshape(base_count, capacity, field_count).transpose(0, 2, 1))
    received = lax.all_to_all(
        jnp.stack(outgoing, axis=1), "base", split_axis=0, concat_axis=0, tiled=True
    )
    extended = []
    for channel in range(channels_here):
        slot_fields = (
            received[:, channel].transpose(1, 0, 2).reshape(field_count, base_count * capacity)
        )
        extended.append(grid_rows(slot_fields, 0, tile_rows + KW).reshape(tile_rows + KW, 2, G))
    extended = jnp.stack(extended, axis=1)
    incoming = passed_along(extended[tile_rows:], "base", 1)
    grid_tile = extended[:tile_rows].at[:KW].add(incoming)
    halves = row_transform(grid_tile, dft_table, tile_rows, channels_here)
    columns = lax.all_to_all(halves, "base", split_axis=3, concat_axis=1, tiled=True)
    stacked = to_columns(columns, tile_rows, channels_here)
    spectra = contract_slots(dft_table, stacked)
    normalizer = 1.0 / (channels_here * freq_count * slots * base_count)
    squared = spectra[:G] * spectra[:G] + spectra[G:] * spectra[G:]
    power_part = jnp.sum(squared.reshape(G, channels_here, tile_rows), axis=1) * normalizer
    bins_here = bin_map.T
    share_rows = G // freq_count
    share_start = lax.axis_index("freq") * share_rows
    power_share = lax.psum_scatter(power_part, "freq", scatter_dimension=0, tiled=True)
    bins_share = lax.dynamic_slice_in_dim(bins_here, share_start, share_rows, 0)
    bin_sums_local = histogram(jnp.stack([power_share, jnp.ones_like(power_share)]), bins_share)
    totals, counts = lax.psum((bin_sums_local[0], bin_sums_local[1]), ("freq", "base"))
    return (power_share, totals / counts)


def solution(mesh):
    in_specs = (
        P(None, "freq", "base"),
        P("freq", "base", None),
        P("freq", "base"),
        P("freq", "base"),
        P(None, "freq", "base"),
        P(),
        P("freq", "base"),
        P("base", None),
    )
    out_specs = (P("freq", "base"), P())
    return jax.shard_map(
        per_device, mesh=mesh, in_specs=in_specs, out_specs=out_specs, check_vma=False
    )
```

profile of v0, /device:TPU:0, one launch (start us, length us, event | category | flops | bytes accessed | tf_op | source)
XLA Modules:
  0.0 432.0 jit_solution(2849988539622279299)
XLA Ops:
  7.2 0.8 iota_compare_fusion.8
  8.0 0.7 broadcast_compare_fusion
  8.7 0.7 copy.136
  9.4 0.7 fusion.149
  10.1 2.4 reduce-window.6
  12.5 0.3 slice_reduce_fusion
  12.8 0.4 reduce-window.9
  13.2 0.1 broadcast_add_fusion
  13.3 0.8 subtract_convert_fusion
  14.1 0.7 fusion.177
  14.8 1.6 convolution_bitcast_fusion
  16.4 0.7 convert_element_type.75
  17.1 0.7 compare_select_fusion.2
  17.9 0.3 concatenate.24
  18.1 0.1 copy.61
  18.3 1.8 scatter_custom_fusion
  20.1 0.2 copy.62
  20.3 0.1 copy.63
  20.5 1.8 scatter_custom_fusion.1
  22.3 0.2 copy.64
  22.6 0.8 copy.65
  23.4 6.3 %all-to-all-start = ((f32[4,2,20,256]{3,1,2,0:T(2,128)}), f32[4,2,20,256]{3,1,2,0:T(2,128)S(1)}, u32[]{:S(2)}, u32[]{:S(2)}) async-start(f32[4,2,20,256]{3,1,2,0:T(2,128)} %copy.65), calls=%async_computation | async-start | bytes 327680 | tf_op jit(solution)/shard_map/all_to_all | solution.py:153
  29.7 17.5 %fusion.36 = (f32[1024,1024]{1,0:T(8,128)}, f32[1024,1024]{1,0:T(8,128)}) fusion(), kind=kLoop, calls=%fused_computation.59 | loop fusion | flops 14680064 | bytes 8388608 | tf_op jit(solution)/shard_map/sin | solution.py:87
  47.3 16.5 %fusion.38 = f32[1024,1024]{1,0:T(8,128)} fusion(), kind=kLoop, calls=%fused_computation.61 | loop fusion | flops 15728640 | bytes 4194304 | tf_op jit(solution)/shard_map/neg | solution.py:89
  63.7 0.1 fusion.176
  64.2 4.4 %broadcast_multiply_fusion.1 = (f32[1024,1024]{1,0:T(8,128)S(1)}, f32[1024,1024]{1,0:T(8,128)S(1)}) fusion(f32[1024]{0:T(1024)S(1)} %bitcast.240, f32[1024]{0:T(1024)S(1)} %bitcast.258, f32[1024]{0:T(1024)S(1)} %bitcast.256, f32[1024]{0:T(1024)S(1)} %bitcast.254, f32[1024]{0:T(1024)S(1)} %bitcast.252, f32[1024]{0:T(1024)S(1)} %bitcast.250, ...), kind=kLoop, calls=%fused_computation.56 | loop fusion | flops 27262976 | bytes 8433664 | tf_op jit(solution)/shard_map/mul | solution.py:71
  68.6 10.1 %fusion.9 = f32[264,2048]{1,0:T(8,128)} fusion(f32[1024,1024]{1,0:T(8,128)S(1)} %get-tuple-element.127, f32[1024,1024]{1,0:T(8,128)S(1)} %get-tuple-element.126, f32[1024]{0:T(1024)S(1)} %bitcast.276, f32[1024]{0:T(1024)S(1)} %bitcast.274, f32[1024]{0:T(1024)S(1)} %bitcast.272, f32[1024]{0:T(1024)S(1)} %bitcast.270, f32[1024]{0:T(1024)S(1)} %bitcast.284, ...), kind=kOutput, calls=%fused_computation.18 | convolution fusion | flops 6652362752 | bytes 10588160 | tf_op jit(solution)/shard_map/dot_general | solution.py:75
  78.7 3.2 stack_reshape.7
  82.1 4.1 broadcast_multiply_fusion.3
  86.2 10.1 %fusion.5 = f32[264,2048]{1,0:T(8,128)} fusion(f32[1024,1024]{1,0:T(8,128)S(1)} %get-tuple-element.129, f32[1024,1024]{1,0:T(8,128)S(1)} %get-tuple-element.128, f32[1024]{0:T(1024)S(1)} %bitcast.285, f32[1024]{0:T(1024)S(1)} %bitcast.283, f32[1024]{0:T(1024)S(1)} %bitcast.281, f32[1024]{0:T(1024)S(1)} %bitcast.279, f32[1024]{0:T(1024)S(1)} %bitcast.277, ...), kind=kOutput, calls=%fused_computation.14 | convolution fusion | flops 6652362752 | bytes 10588160 | tf_op jit(solution)/shard_map/dot_general | solution.py:75
  96.3 4.1 stack_reshape.6
  100.4 2.5 constant_dynamic-update-slice_fusion.1
  102.9 0.9 constant_dynamic-update-slice_fusion
  103.8 3.9 collective-permute-start
  107.8 12.9 %maximum_maximum_fusion = f32[2048,2048]{1,0:T(8,128)} fusion(f32[1024,1024]{1,0:T(8,128)S(1)} %copy-done.3, f32[1024,1024]{1,0:T(8,128)S(1)} %copy-done.1, f32[1024,1024]{1,0:T(8,128)} %fusion.38), kind=kLoop, calls=%fused_computation.9 | loop fusion | flops 12582912 | bytes 29360128 | tf_op jit(solution)/shard_map/concatenate | solution.py:88
  120.7 3.4 slice.363
  124.1 0.7 fusion.144
  124.8 6.7 %reshape.405 = f32[256,2,2048]{2,0,1:T(8,128)} reshape(f32[256,2,2,1024]{3,2,0,1:T(2,128)} %fusion.144) | data formatting | bytes 8388608 | tf_op jit(solution)/shard_map/reshape.292
  131.5 16.9 %fusion.39 = f32[1,256,2,1024]{3,1,2,0:T(8,128)S(1)} fusion(f32[256,2,2048]{2,0,1:T(8,128)} %reshape.405, f32[2048,2048]{1,0:T(8,128)} %maximum_maximum_fusion), kind=kOutput, calls=%fused_computation.62 | convolution fusion | flops 12884901888 | bytes 14680064 | tf_op jit(solution)/shard_map/dot_general | solution.py:97
  148.4 16.3 %fusion.40 = f32[1,256,2,1024]{3,1,2,0:T(8,128)S(1)} fusion(f32[256,2,2048]{2,0,1:T(8,128)S(1)} %copy-done.5, f32[2048,2048]{1,0:T(8,128)} %maximum_maximum_fusion), kind=kOutput, calls=%fused_computation.63 | convolution fusion | flops 12884901888 | bytes 14680064 | tf_op jit(solution)/shard_map/dot_general | solution.py:98
  164.7 2.3 pad_maximum_fusion
  167.0 7.2 %copy.68 = f32[2,256,2,1024]{1,2,0,3:T(2,128)} copy(f32[2,256,2,1024]{3,1,2,0:T(8,128)} %pad_maximum_fusion) | data formatting | bytes 8388608 | tf_op jit(solution)/shard_map/stack | solution.py:95
  174.2 98.3 %all_to_all.20 = f32[2,256,2,1024]{1,2,0,3:T(2,128)} all-to-all(f32[2,256,2,1024]{1,2,0,3:T(2,128)} %copy.68), channel_id=1, replica_groups=mesh['freq'=8,'base'=4] {'base'}, dimensions={3} | all-to-all | bytes 8388608 | tf_op jit(solution)/shard_map/all_to_all | solution.py:166
  272.5 10.9 %copy.69 = f32[2,256,2,4,256]{4,2,1,3,0:T(2,128)} copy(f32[2,256,2,4,256]{1,2,0,4,3:T(2,128)} %bitcast.228) | data formatting | bytes 8388608 | tf_op jit(solution)/shard_map/all_to_all | solution.py:166
  283.4 4.9 %copy.120 = f32[256,8,2,256]{3,1,2,0:T(8,128)} copy(f32[256,8,2,256]{3,2,1,0:T(2,128)} %bitcast.229) | data formatting | bytes 8388608
  288.3 1.3 copy-done.4
  289.6 33.1 %fusion.175 = f32[2048,512]{0,1:T(8,128)S(1)} fusion(f32[2048,512]{1,0:T(8,128)} %bitcast.231, f32[1024,1024]{1,0:T(8,128)S(1)} %copy-done.4, f32[1024,1024]{1,0:T(8,128)S(1)} %copy-done.2, f32[1024,1024]{1,0:T(8,128)} %fusion.38), kind=kOutput, calls=%fused_computation.257 | convolution fusion | flops 25782386688 | bytes 20971520 | tf_op jit(solution)/shard_map/dot_general | solution.py:75
  322.7 0.4 fusion.35
  323.2 1.2 reduce_sum.19
  324.4 2.3 broadcast_multiply_fusion.4
  326.8 0.1 copy.71
  326.9 0.1 reshape.409
  327.0 34.9 %reduce-scatter.2.cloned.1.call-done = f32[128,256]{0,1:T(8,128)} async-done(((f32[1024,256]{0,1:T(8,128)}), f32[128,256]{0,1:T(8,128)}) %reduce-scatter.2.cloned.1.call-update) | async-done | bytes 131088 | tf_op jit(solution)/shard_map/reduce_scatter | solution.py:175
  361.9 1.0 copy.79
  362.9 0.2 reshape.408
  363.1 21.1 %while.12 = (s32[]{:T(128)}, f32[2,512]{1,0:T(2,128)S(1)}, f32[2,2,16384]{2,0,1:T(2,128)S(1)}, s32[2,16384]{1,0:T(2,128)S(1)}, s32[]{:T(128)}, /*index=5*/s32[]{:T(128)}) while((s32[]{:T(128)}, f32[2,512]{1,0:T(2,128)S(1)}, f32[2,2,16384]{2,0,1:T(2,128)S(1)}, s32[2,16384]{1,0:T(2,128)S(1)}, s32[]{:T(128)}, ...), condition=%wide.region_8.9_spmd.clone, body=%wide.region_7.8_spmd.clone.sunk | while | flops 209717248 | bytes 598103 | solution.py:123
  363.1 0.1 constant_dynamic-slice_fusion.5
  363.3 0.1 constant_dynamic-slice_fusion.4
  363.4 10.3 %fusion.183 = f32[2,512]{1,0:T(2,128)S(1)} fusion(s32[16384]{0:T(1024)S(1)} %bitcast.235, f32[1,2,16384]{2,0,1:T(1,128)S(1)} %constant_dynamic-slice_fusion.5, f32[2,512]{1,0:T(2,128)S(1)} %get-tuple-element.176, pred[]{:T(512)S(6)} %compare.11), kind=kOutput, calls=%fused_computation.5.clone.1 | convolution fusion | flops 209717248 | bytes 204801 | tf_op jit(solution)/shard_map/while/body/eval_jaxpr/dot_general | solution.py:121
  373.7 0.1 constant_dynamic-slice_fusion.5
  373.9 10.3 %fusion.183 = f32[2,512]{1,0:T(2,128)S(1)} fusion(s32[16384]{0:T(1024)S(1)} %bitcast.235, f32[1,2,16384]{2,0,1:T(1,128)S(1)} %constant_dynamic-slice_fusion.5, f32[2,512]{1,0:T(2,128)S(1)} %get-tuple-element.176, pred[]{:T(512)S(6)} %compare.11), kind=kOutput, calls=%fused_computation.5.clone.1 | convolution fusion | flops 209717248 | bytes 204801 | tf_op jit(solution)/shard_map/while/body/eval_jaxpr/dot_general | solution.py:121
  384.2 39.3 %all-reduce.1 = (f32[512]{0:T(512)S(1)}, f32[512]{0:T(512)S(1)}) all-reduce(f32[512]{0:T(512)S(1)} %bitcast.265, f32[512]{0:T(512)S(1)} %bitcast.264), channel_id=1, replica_groups=mesh['freq'=8,'base'=4] {'freq','base'}, use_global_device_ids=true, to_apply=%region_9.10 | all-reduce | flops 1024 | bytes 8192 | tf_op jit(solution)/shard_map/psum | solution.py:178
  423.5 0.6 div.3
  424.1 0.8 copy.73
  (77 shorter events, 0.5 us)
Async XLA Ops:
  7.2 319.6 %copy-start = (s32[256,1024]{1,0:T(8,128)S(1)}, s32[256,1024]{1,0:T(8,128)}, u32[]{:S(2)}) copy-start(s32[256,1024]{1,0:T(8,128)} %param.19) | copy-start | bytes 3145732
  23.4 40.4 %all-to-all-start = ((f32[4,2,20,256]{3,1,2,0:T(2,128)}), f32[4,2,20,256]{3,1,2,0:T(2,128)S(1)}, u32[]{:S(2)}, u32[]{:S(2)}) async-start(f32[4,2,20,256]{3,1,2,0:T(2,128)} %copy.65), calls=%async_computation | async-start | bytes 327680 | tf_op jit(solution)/shard_map/all_to_all | solution.py:153
  29.7 332.2 %reduce-scatter.2.cloned.1.call-start = ((), (), s32[]{:S(2)}) async-start(), calls=%async_computation.3 | async-start | bytes 1179648 | tf_op jit(solution)/shard_map/reduce_scatter | solution.py:175
  100.4 7.4 %copy-start.1 = (f32[1024,1024]{1,0:T(8,128)S(1)}, f32[1024,1024]{1,0:T(8,128)}, u32[]{:S(2)}) copy-start(f32[1024,1024]{1,0:T(8,128)} %get-tuple-element.142) | copy-start | bytes 12582916
  100.4 7.4 %copy-start.3 = (f32[1024,1024]{1,0:T(8,128)S(1)}, f32[1024,1024]{1,0:T(8,128)}, u32[]{:S(2)}) copy-start(f32[1024,1024]{1,0:T(8,128)} %get-tuple-element.143) | copy-start | bytes 12582916
  103.8 20.3 %collective-permute-start = (f32[8,2,2,1024]{3,2,0,1:T(2,128)S(1)}, f32[8,2,2,1024]{3,2,0,1:T(2,128)S(1)}, u32[]{:S(2)}, u32[]{:S(2)}) collective-permute-start(f32[8,2,2,1024]{3,2,0,1:T(2,128)S(1)} %slice.365), channel_id=1, source_target_pairs={{0,1},{1,2},{2,3},{4,5},{5,6},{6,7},{8,9},{9,10},{10,11},{12,13},{... | collective-permute-start | bytes 393224 | tf_op jit(solution)/shard_map/ppermute | solution.py:19
  131.5 16.9 %copy-start.5 = (f32[256,2,2048]{2,0,1:T(8,128)S(1)}, f32[256,2,2048]{2,0,1:T(8,128)}, u32[]{:S(2)}) copy-start(f32[256,2,2048]{2,0,1:T(8,128)} %reshape.405) | copy-start | bytes 12582916
  283.4 4.9 %copy-start.2 = (f32[1024,1024]{1,0:T(8,128)S(1)}, f32[1024,1024]{1,0:T(8,128)}, u32[]{:S(2)}) copy-start(f32[1024,1024]{1,0:T(8,128)} %get-tuple-element.142) | copy-start | bytes 12582916
  283.4 6.2 %copy-start.4 = (f32[1024,1024]{1,0:T(8,128)S(1)}, f32[1024,1024]{1,0:T(8,128)}, u32[]{:S(2)}) copy-start(f32[1024,1024]{1,0:T(8,128)} %get-tuple-element.143) | copy-start | bytes 12582916
  363.1 61.0 %copy-start.6 = (f32[128,256]{0,1:T(8,128)S(1)}, f32[128,256]{0,1:T(8,128)}, u32[]{:S(2)}) copy-start(f32[128,256]{0,1:T(8,128)} %reduce-scatter.2.cloned.1.call-done) | copy-start | bytes 393220
Sparse Core Ops, SparseCore 0:
  326.8 35.0 reduce-scatter.1
where the time goes:
time: 440 us; the launch traced here: 432 us
  blocking collectives  138 us (31%)
  matrix products  109 us (25%)
  other arithmetic  70.4 us (16%)
  local copies, waits for them, and re-layouts  55.1 us (13%)
  waiting for transfers between devices  35 us (8%)
  between operations  14.9 us (3%)
  starting transfers between devices  10.3 us (2%)
    all_to_all x1, blocking collectives, per_device(): lax.all_to_all(halves, 'base', split_axis=3, concat_axis=1, tiled=True)  98.3 us
    dot_general x3, matrix products, contract_slots(): lax.dot_general(upper, lower, (((0,), (0,)), ((), ())), precision=HIGHEST...  53.3 us
    psum x1, blocking collectives, per_device(): lax.psum((bin_sums_local[0], bin_sums_local[1]), ('freq', 'base'))  39.3 us
    reduce_scatter x1, waiting for transfers between devices, per_device(): lax.psum_scatter(power_part, 'freq', scatter_dimension=0, tiled=True)  34.9 us
    dot_general x2, matrix products, add_block(): jnp.dot(values, onehot, precision=HIGHEST_PRECISION)  20.6 us
    sin x1, other arithmetic, dft_matrix(): sine = jnp.sin(angle)  17.5 us
    dot_general x1, matrix products, row_transform(): jnp.dot(flat_rows, dft_table[:, :G], precision=HIGHEST_PRECISION)  16.9 us
    neg x1, other arithmetic, dft_matrix(): -sine  16.5 us
  transfers between devices with their start and end apart: 3, of which 1 were waited for; matrix products, arithmetic and copies ran while one was open for 12% of the time, Pallas kernels for 0%

commit v1 on v0

v1 whole, which is shorter than its diff:
```python
import functools

import jax
import jax.numpy as jnp
import numpy as np
from jax import lax
from jax.experimental import pallas as pl
from jax.experimental.pallas import tpu as pltpu
from jax.sharding import PartitionSpec as P

G = 1024
NBINS = 512
KW = 8
RADIX = 4
SUB = G // RADIX
CHUNK = 256
LANES = 128
V_LOW = 32
V_HIGH = G // V_LOW
BIN_LOW = 16
BIN_HIGH = NBINS // BIN_LOW
F32 = jnp.float32
BF16 = jnp.bfloat16


def np_split(x):
    high = x.astype(np.float32).astype(jnp.bfloat16)
    low = (x - high.astype(np.float64)).astype(np.float32).astype(jnp.bfloat16)
    return high, low


def split(x):
    high = x.astype(BF16)
    return high, (x - high.astype(F32)).astype(BF16)


def row_dft_tables():
    k = np.arange(SUB)[:, None]
    tables = []
    for first in range(RADIX):
        u = RADIX * np.arange(SUB)[None, :] + first
        angle = 2 * np.pi * (k * u % G) / G
        high, low = np_split(np.concatenate([np.cos(angle), np.sin(angle)], 0))
        tables.append(np.concatenate([high, low], 1))
    return np.stack(tables)


def phases(cells, peers):
    columns = np.arange(G)[:, None]
    angle = 2 * np.pi * (columns * cells[None, :] % G) / G
    width = G // peers
    shape = (peers, width, len(cells))
    return np.cos(angle).reshape(shape), np.sin(angle).reshape(shape)


def column_tables(peers):
    cosine, sine = phases(V_LOW * np.arange(V_HIGH), peers)
    coarse = np.concatenate(
        [np.concatenate([cosine, sine], 2), np.concatenate([-sine, cosine], 2)], 1
    )
    high, low = np_split(coarse)
    coarse = np.concatenate([high, low, high], 2)
    cosine, sine = phases(np.arange(V_LOW), peers)
    high, low = np_split(np.concatenate([cosine, -sine], 1))
    fine = np.concatenate([high, low], 2)
    cosine, sine = phases(np.arange(KW), peers)
    taps = np.concatenate([cosine, -sine], 1).astype(np.float32)
    return coarse, fine, taps


def dot(a, b, transposed=False, **kw):
    dims = (((1,), (1,)), ((), ())) if transposed else (((1,), (0,)), ((), ()))
    return lax.dot_general(a, b, dims, preferred_element_type=F32, **kw)


def image_kernel(
    base_ref, live_ref, gathered_ref, kernel_ref, row_ref, coarse_ref, fine_ref, tap_ref,
    out_ref, packed_ref, spectrum_ref, kernel_halves_ref, grid_ref, *, normalizer,
):
    channel = pl.program_id(0)
    peers, _, _, slots = gathered_ref.shape
    width = out_ref.shape[1]
    table_rows = kernel_ref.shape[1]

    @pl.when(channel == 0)
    def _():
        high, low = split(
            dot(tap_ref[...], kernel_ref[...], precision=lax.Precision.HIGHEST)
        )
        spectrum_ref[...] = jnp.concatenate([high, low], axis=1)
        high = kernel_ref[...].astype(BF16).astype(F32)
        kernel_halves_ref[...] = jnp.concatenate([high, kernel_ref[...] - high], axis=0)

    packed_ref[...] = jnp.zeros_like(packed_ref)
    offset = jnp.int32(0)
    lane = lax.broadcasted_iota(jnp.int32, (8, slots + LANES), 1)
    for peer in range(peers):
        live = live_ref[peer, channel]
        block = offset // LANES
        within = offset - block * LANES
        fields = jnp.concatenate(
            [gathered_ref[peer, 0], jnp.zeros((8, LANES), F32)], axis=1
        )
        fields = pltpu.roll(fields, within, 1)
        kept = (lane >= within) & (lane < within + live)
        window = pl.ds(pl.multiple_of(block * LANES, LANES), slots + LANES)
        packed_ref[:, window] = packed_ref[:, window] + jnp.where(kept, fields, 0.0)
        offset = offset + live

    grid_ref[...] = jnp.zeros_like(grid_ref)

    def add_chunk(index, carry):
        fields = packed_ref[:, pl.ds(pl.multiple_of(index * CHUNK, CHUNK), CHUNK)]
        real, imag = fields[0:1], fields[1:2]
        cells = fields[2:6].astype(jnp.int32)
        u_cell, v_cell, index_u, index_v = cells[0:1], cells[1:2], cells[2:3], cells[3:4]
        table_row = lax.broadcasted_iota(jnp.int32, (table_rows, CHUNK), 0)
        chosen_v = jnp.where(table_row == index_v, 1.0, 0.0).astype(BF16)
        footprint = dot(spectrum_ref[...], jnp.concatenate([chosen_v, chosen_v], axis=0))
        high_row = lax.broadcasted_iota(jnp.int32, (V_HIGH, CHUNK), 0)
        at_coarse = high_row == v_cell // V_LOW
        values = jnp.concatenate(
            [jnp.where(at_coarse, real, 0.0), jnp.where(at_coarse, imag, 0.0)], axis=0
        )
        high, low = split(values)
        coarse = dot(coarse_ref[...], jnp.concatenate([high, high, low], axis=0))
        low_row = lax.broadcasted_iota(jnp.int32, (V_LOW, CHUNK), 0)
        at_fine = jnp.where(low_row == v_cell % V_LOW, 1.0, 0.0).astype(BF16)
        fine = dot(fine_ref[...], jnp.concatenate([at_fine, at_fine], axis=0))
        a_re, a_im = coarse[:width], coarse[width:]
        b_re, b_im = fine[:width], fine[width:]
        c_re = a_re * b_re - a_im * b_im
        c_im = a_re * b_im + a_im * b_re
        d_re, d_im = footprint[:width], footprint[width:]
        column = jnp.concatenate(
            [c_re * d_re - c_im * d_im, c_re * d_im + c_im * d_re], axis=0
        )
        high, low = split(column)
        column = jnp.concatenate([high, low, high], axis=1)

        chosen_u = jnp.where(table_row == index_u, 1.0, 0.0).astype(BF16)
        taps = dot(kernel_halves_ref[...].astype(BF16), chosen_u)
        grid_row = lax.broadcasted_iota(jnp.int32, (SUB, CHUNK), 0)
        rows = []
        for first in range(RADIX):
            tap = (first - u_cell) & (RADIX - 1)
            start = (u_cell + tap - first) // RADIX

            def tap_of(base):
                value = taps[base : base + 1]
                for t in range(1, RADIX):
                    value = jnp.where(tap == t, taps[base + t : base + t + 1], value)
                return value

            at_first = grid_row == start
            at_second = grid_row == start + 1
            halves = []
            for base in (0, KW):
                part = jnp.where(
                    at_first, tap_of(base), jnp.where(at_second, tap_of(base + RADIX), 0.0)
                )
                halves.append(part.astype(BF16))
            rows.append(jnp.concatenate([halves[0], halves[0], halves[1]], axis=1))
        grid_ref[...] += dot(jnp.concatenate(rows, axis=0), column, transposed=True)
        return carry

    lax.fori_loop(0, (offset + CHUNK - 1) // CHUNK, add_chunk, 0)

    parts = []
    for first in range(RADIX):
        high, low = split(grid_ref[first * SUB : (first + 1) * SUB, :])
        table = row_ref[first]
        table = jnp.concatenate([table[:, :SUB], table], axis=1)
        both = dot(table, jnp.concatenate([high, low, high], axis=0))
        re = both[:SUB, :width] + both[SUB:, width:]
        im = both[:SUB, width:] - both[SUB:, :width]
        parts.append((re, im))
    (r0, i0), (r1, i1), (r2, i2), (r3, i3) = parts
    ar, ai, br, bi = r0 + r2, i0 + i2, r0 - r2, i0 - i2
    cr, ci, dr, di = r1 + r3, i1 + i3, r1 - r3, i1 - i3
    images = [
        (ar + cr, ai + ci),
        (br + di, bi - dr),
        (ar - cr, ai - ci),
        (br - di, bi + dr),
    ]
    for block, (re, im) in enumerate(images):
        window = slice(block * SUB, (block + 1) * SUB)
        power = (re * re + im * im) * normalizer

        @pl.when(channel == 0)
        def _():
            out_ref[window, :] = power

        @pl.when(channel != 0)
        def _():
            out_ref[window, :] += power


def image_power(base_index, live, gathered, kernel, normalizer):
    peers, channels, _, slots = gathered.shape
    width = G // peers
    coarse, fine, taps = column_tables(peers)
    table_rows = kernel.shape[0]
    whole = lambda shape: pl.BlockSpec(shape, lambda c, *_: (0,) * len(shape))
    own = lambda x: pl.BlockSpec((None,) + x.shape[1:], lambda c, b, *_: (b[0], 0, 0))
    rows = row_dft_tables()
    spec = pltpu.PrefetchScalarGridSpec(
        num_scalar_prefetch=2,
        grid=(channels,),
        in_specs=[
            pl.BlockSpec((peers, 1, 8, slots), lambda c, *_: (0, c, 0, 0)),
            whole((KW, table_rows)),
            whole(rows.shape),
            own(coarse),
            own(fine),
            own(taps),
        ],
        out_specs=whole((G, width)),
        scratch_shapes=[
            pltpu.VMEM((8, peers * slots + LANES), F32),
            pltpu.VMEM((2 * width, 2 * table_rows), BF16),
            pltpu.VMEM((2 * KW, table_rows), F32),
            pltpu.VMEM((G, 2 * width), F32),
        ],
    )
    return pl.pallas_call(
        functools.partial(image_kernel, normalizer=normalizer),
        grid_spec=spec,
        out_shape=jax.ShapeDtypeStruct((G, width), F32),
        compiler_params=pltpu.CompilerParams(dimension_semantics=("arbitrary",)),
        name="image_power",
    )(base_index, live, gathered, kernel.T, rows, coarse, fine, taps)


def bin_kernel(freq_ref, power_ref, bins_ref, share_ref, sums_ref, bins_t_ref):
    share = power_ref[0]
    for peer in range(1, power_ref.shape[0]):
        share = share + power_ref[peer]
    share_ref[...] = share
    bins_t_ref[...] = bins_ref[...].astype(F32).T
    rows, width = share.shape
    group = 8
    high_row = lax.broadcasted_iota(jnp.int32, (BIN_HIGH, width), 0)
    low_row = lax.broadcasted_iota(jnp.int32, (BIN_LOW, width), 0)

    def add_group(index, running):
        window = pl.ds(pl.multiple_of(index * group, group), group)
        bins = bins_t_ref[window, :].astype(jnp.int32)
        values = share_ref[window, :]
        high = values.astype(BF16).astype(F32)
        rest = values - high
        middle = rest.astype(BF16).astype(F32)
        low = rest - middle
        left, right = [], []
        for row in range(group):
            one = slice(row, row + 1)
            at_high = high_row == bins[one] // BIN_LOW
            at_low = low_row == bins[one] % BIN_LOW
            left.append(jnp.where(at_high, 1.0, 0.0).astype(BF16))
            pieces = [jnp.where(at_low, x[one], 0.0) for x in (high, middle, low)]
            pieces.append(jnp.where(at_low, 1.0, 0.0))
            right.append(jnp.concatenate(pieces, axis=0).astype(BF16))
        if width % LANES == 0:
            left, right = [jnp.concatenate(left, axis=1)], [jnp.concatenate(right, axis=1)]
        for a, b in zip(left, right):
            running = running + dot(a, b, transposed=True)
        return running

    zeros = jnp.zeros((BIN_HIGH, 4 * BIN_LOW), F32)
    sums_ref[...] = lax.fori_loop(0, rows // group, add_group, zeros)


def bin_power(freq_index, received, bin_map):
    peers, rows, width = received.shape
    if rows % LANES:
        bin_map = lax.dynamic_slice_in_dim(bin_map, freq_index[0] * rows, rows, 1)
        freq_index = jnp.zeros_like(freq_index)
    spec = pltpu.PrefetchScalarGridSpec(
        num_scalar_prefetch=1,
        grid=(1,),
        in_specs=[
            pl.BlockSpec((peers, rows, width), lambda i, f: (0, 0, 0)),
            pl.BlockSpec((width, rows), lambda i, f: (0, f[0])),
        ],
        out_specs=[
            pl.BlockSpec((rows, width), lambda i, f: (0, 0)),
            pl.BlockSpec((BIN_HIGH, 4 * BIN_LOW), lambda i, f: (0, 0)),
        ],
        scratch_shapes=[pltpu.VMEM((rows, width), F32)],
    )
    return pl.pallas_call(
        bin_kernel,
        grid_spec=spec,
        out_shape=[
            jax.ShapeDtypeStruct((rows, width), F32),
            jax.ShapeDtypeStruct((BIN_HIGH, 4 * BIN_LOW), F32),
        ],
        name="bin_power",
    )(freq_index, received, bin_map)


def sent_to_all(x, axis):
    copies = jnp.broadcast_to(x[None], (lax.axis_size(axis),) + x.shape)
    return lax.all_to_all(copies, axis, split_axis=0, concat_axis=0)


def per_device(visibility, tile_of, u_within, v_cell, kernel_index, kernel, live_count, bin_map):
    base_count = lax.axis_size("base")
    freq_count = lax.axis_size("freq")
    tile_rows = G // base_count
    channels_here, slots = visibility.shape[1:]
    u_cell = jnp.minimum(tile_of[:, :, 0] * tile_rows + u_within, G - KW)
    cells = jnp.stack([u_cell, v_cell, kernel_index[0], kernel_index[1]]).astype(F32)
    counts = jnp.broadcast_to(live_count.astype(F32)[None], (1, channels_here, slots))
    fields = jnp.concatenate([visibility, cells, counts, jnp.zeros_like(counts)], axis=0)
    gathered = sent_to_all(fields.transpose(1, 0, 2), "base")
    live = gathered[:, :, 6, 0].astype(jnp.int32)
    normalizer = 1.0 / (channels_here * freq_count * slots * base_count)
    power_part = image_power(
        lax.axis_index("base")[None], live, gathered, kernel, normalizer
    )
    blocks = power_part.reshape(freq_count, G // freq_count, -1)
    received = lax.all_to_all(blocks, "freq", split_axis=0, concat_axis=0)
    power_share, sums = bin_power(lax.axis_index("freq")[None], received, bin_map)
    sums = sums.reshape(BIN_HIGH, 4, BIN_LOW)
    sums = jnp.stack([sums[:, 0] + sums[:, 1] + sums[:, 2], sums[:, 3]]).reshape(2 * NBINS)
    sums = jnp.sum(sent_to_all(sums, ("freq", "base")), axis=0)
    return power_share, sums[:NBINS] / sums[NBINS:]


def solution(mesh):
    in_specs = (
        P(None, "freq", "base"),
        P("freq", "base", None),
        P("freq", "base"),
        P("freq", "base"),
        P(None, "freq", "base"),
        P(),
        P("freq", "base"),
        P("base", None),
    )
    out_specs = (P("freq", "base"), P())
    return jax.shard_map(
        per_device, mesh=mesh, in_specs=in_specs, out_specs=out_specs, check_vma=False
    )
```

time: 440 us -> 81 us (0.18); the launches traced: 432 us -> 80.4 us
  blocking collectives: 138 us -> 10.1 us
  matrix products: 109 us -> 0 us
  other arithmetic: 70.4 us -> 3.56 us
  local copies, waits for them, and re-layouts: 55.1 us -> 3.58 us
  Pallas kernels: 0 us -> 31 us
  between operations: 14.9 us -> 0.67 us
  waiting for transfers between devices: 35 us -> 21.5 us
    dot_general x8 -> x0, matrix products: 109 us -> none  [the longest x3 53.3 us: contract_slots(): lax.dot_general(upper, lower, (((0,), (0,)), ((), ())), precision=HIGHEST...]
    all_to_all x1, blocking collectives: 98.3 us -> 10.1 us  [sent_to_all(): return lax.all_to_all(copies, axis, split_axis=0, concat_axis=0)]
    psum x1 -> x0, blocking collectives: 39.3 us -> none  [per_device(): lax.psum((bin_sums_local[0], bin_sums_local[1]), ('freq', 'base'))]
    reduce_scatter x1 -> x0, waiting for transfers between devices: 34.9 us -> none  [per_device(): lax.psum_scatter(power_part, 'freq', scatter_dimension=0, tiled=True)]
    pallas_call x0 -> x2, Pallas kernels: none -> 31 us  [the longest x1 25.5 us: image_power(): pl.pallas_call(functools.partial(image_kernel, normalizer=normalizer), gr...]
    another operation x9 -> x1, local copies, waits for them, and re-layouts: 23.1 us -> 0.07 us  [per_device(): jnp.stack([sums[:, 0] + sums[:, 1] + sums[:, 2], sums[:, 3]])]
    all_to_all x1 -> x2, waiting for transfers between devices: 0.01 us -> 21.5 us  [the longest x1 15.4 us: per_device(): received = lax.all_to_all(blocks, 'freq', split_axis=0, concat_axis=0)]
    sin x1 -> x0, other arithmetic: 17.5 us -> none  [dft_matrix(): sine = jnp.sin(angle)]
  transfers between devices with their start and end apart: 3 -> 2, of which waited for: 1 -> 2; matrix products, arithmetic and copies ran while one was open for 12% -> 0% of each run, Pallas kernels for 0% -> 0%
where the time goes in v1:
time: 81 us; the launch traced here: 80.4 us
  Pallas kernels  31 us (38%)
  waiting for transfers between devices  21.5 us (27%)
  starting transfers between devices  10.1 us (12%)
  blocking collectives  10.1 us (12%)
  local copies, waits for them, and re-layouts  3.58 us (4%)
  other arithmetic  3.56 us (4%)
    pallas_call x1, Pallas kernels, image_power(): pl.pallas_call(functools.partial(image_kernel, normalizer=normalizer), gr...  25.5 us
    all_to_all x1, waiting for transfers between devices, per_device(): received = lax.all_to_all(blocks, 'freq', split_axis=0, concat_axis=0)  15.4 us
    all_to_all x1, blocking collectives, sent_to_all(): return lax.all_to_all(copies, axis, split_axis=0, concat_axis=0)  10.1 us
    all_to_all x1, starting transfers between devices, sent_to_all(): return lax.all_to_all(copies, axis, split_axis=0, concat_axis=0)  6.35 us
    all_to_all x1, waiting for transfers between devices, sent_to_all(): return lax.all_to_all(copies, axis, split_axis=0, concat_axis=0)  6.07 us
    pallas_call x1, Pallas kernels, bin_power(): pl.pallas_call(bin_kernel, grid_spec=spec, out_shape=[jax.ShapeDtypeStruc...  5.49 us
    all_to_all x1, starting transfers between devices, per_device(): received = lax.all_to_all(blocks, 'freq', split_axis=0, concat_axis=0)  3.71 us
  transfers between devices with their start and end apart: 2, of which 2 were waited for; matrix products, arithmetic and copies ran while one was open for 0% of the time, Pallas kernels for 0%

profile of v1, /device:TPU:0, one launch (start us, length us, event | category | flops | bytes accessed | tf_op | source)
XLA Modules:
  0.0 80.4 jit_solution(9145872009831932131)
XLA Ops:
  0.6 0.7 convert_bitcast_fusion
  1.3 0.1 pad.5.clone
  1.4 0.7 fusion.2
  2.1 0.7 add_convert_fusion
  2.8 0.1 broadcast_in_dim.33
  2.9 0.8 maximum_bitcast_fusion
  3.6 0.7 broadcast_in_dim.35
  4.3 6.3 %all-to-all-start = ((f32[4,2,8,512]{3,2,1,0:T(8,128)}), f32[4,2,8,512]{3,2,1,0:T(8,128)S(1)}, u32[]{:S(2)}, u32[]{:S(2)}) async-start(f32[4,2,8,512]{3,2,1,0:T(8,128)} %broadcast_in_dim.35), calls=%async_computation | async-start | bytes 262144 | tf_op jit(solution)/shard_map/all_to_all | solution.py:305
  10.7 6.1 %all-to-all-done.gathered_ref = f32[4,2,8,512]{3,2,1,0:T(8,128)S(1)} async-done(((f32[4,2,8,512]{3,2,1,0:T(8,128)}), f32[4,2,8,512]{3,2,1,0:T(8,128)S(1)}, u32[]{:S(2)}, u32[]{:S(2)}) %all-to-all-start) | async-done | bytes 131104 | tf_op jit(solution)/shard_map/all_to_all | solution.py:305
  16.7 0.0 copy-start.1
  16.7 0.1 copy.42
  16.8 0.7 copy.43.live_ref
  17.5 0.0 copy-done.1
  17.5 25.5 %image_power.1 = f32[1024,256]{1,0:T(8,128)} custom-call(s32[1]{0:T(128)} %bitcast.1.base_ref, s32[4,2]{1,0:T(4,128)} %copy.43.live_ref, f32[4,2,8,512]{3,2,1,0:T(8,128)} %copy-done.1, f32[8,128]{1,0:T(8,128)} %bitcast.26, bf16[4,512,512]{2,1,0:T(8,128)(2,1)} %constant.24.clone.row_ref, bf16[4,512,192]{2,1,0:T(8,128)(2,1)} %constant.25.clone.coarse_ref, ...), custom_call_target="tpu_custom_call" | custom-call | tf_op jit(solution)/shard_map/image_power/pallas_call | solution.py:227
  43.1 3.7 %all-to-all-start.1 = ((f32[8,128,256]{2,1,0:T(8,128)}), f32[8,128,256]{2,1,0:T(8,128)S(1)}, u32[]{:S(2)}, u32[]{:S(2)}) async-start(f32[8,128,256]{2,1,0:T(8,128)} %bitcast.24), calls=%async_computation.1 | async-start | bytes 2097152 | tf_op jit(solution)/shard_map/all_to_all | solution.py:324
  46.8 15.4 %all-to-all-done.1.power_ref = f32[8,128,256]{2,1,0:T(8,128)S(1)} async-done(((f32[8,128,256]{2,1,0:T(8,128)}), f32[8,128,256]{2,1,0:T(8,128)S(1)}, u32[]{:S(2)}, u32[]{:S(2)}) %all-to-all-start.1) | async-done | bytes 1048608 | tf_op jit(solution)/shard_map/all_to_all | solution.py:324
  62.1 0.0 copy-start
  62.1 1.0 %copy-done = f32[8,128,256]{2,1,0:T(8,128)} copy-done((f32[8,128,256]{2,1,0:T(8,128)}, f32[8,128,256]{2,1,0:T(8,128)S(1)}, u32[]{:S(2)}) %copy-start) | copy-done | bytes 1048600
  63.1 5.5 %bin_power.1 = (f32[128,256]{1,0:T(8,128)}, f32[32,64]{1,0:T(8,128)}) custom-call(s32[1]{0:T(128)} %bitcast.freq_ref, f32[8,128,256]{2,1,0:T(8,128)} %copy-done, s32[256,1024]{1,0:T(8,128)} %bins_ref.1), custom_call_target="tpu_custom_call" | custom-call | tf_op jit(solution)/shard_map/bin_power/pallas_call | solution.py:292
  68.6 0.8 copy.44
  69.4 0.1 copy.45
  69.5 0.1 broadcast_in_dim.36
  69.6 0.1 broadcast_in_dim.37
  69.7 10.1 %all_to_all.16 = f32[32,1,1024]{2,1,0:T(1,128)S(1)} all-to-all(f32[32,1,1024]{2,1,0:T(1,128)S(1)} %broadcast_in_dim.37), channel_id=1, replica_groups=mesh['freq'=8,'base'=4] {'freq','base'}, dimensions={0} | all-to-all | bytes 262144 | tf_op jit(solution)/shard_map/all_to_all | solution.py:305
  79.7 0.1 reduce_sum.9
  79.8 0.6 slice_divide_fusion
  (4 shorter events, 0.0 us)
Async XLA Ops:
  4.3 12.4 %all-to-all-start = ((f32[4,2,8,512]{3,2,1,0:T(8,128)}), f32[4,2,8,512]{3,2,1,0:T(8,128)S(1)}, u32[]{:S(2)}, u32[]{:S(2)}) async-start(f32[4,2,8,512]{3,2,1,0:T(8,128)} %broadcast_in_dim.35), calls=%async_computation | async-start | bytes 262144 | tf_op jit(solution)/shard_map/all_to_all | solution.py:305
  16.7 0.8 copy-start.1
  43.1 19.1 %all-to-all-start.1 = ((f32[8,128,256]{2,1,0:T(8,128)}), f32[8,128,256]{2,1,0:T(8,128)S(1)}, u32[]{:S(2)}, u32[]{:S(2)}) async-start(f32[8,128,256]{2,1,0:T(8,128)} %bitcast.24), calls=%async_computation.1 | async-start | bytes 2097152 | tf_op jit(solution)/shard_map/all_to_all | solution.py:324
  62.1 1.0 %copy-start = (f32[8,128,256]{2,1,0:T(8,128)}, f32[8,128,256]{2,1,0:T(8,128)S(1)}, u32[]{:S(2)}) copy-start(f32[8,128,256]{2,1,0:T(8,128)S(1)} %all-to-all-done.1.power_ref) | copy-start | bytes 3145732

commit v2 on v1

--- a/solution.py
+++ b/solution.py
@@ -12,12 +12,15 @@
 NBINS = 512
 KW = 8
 RADIX = 4
+TILES = 4
+WINDOW = 72
+BLOCK = 264
 SUB = G // RADIX
 CHUNK = 256
 LANES = 128
 V_LOW = 32
 V_HIGH = G // V_LOW
-BIN_LOW = 16
+BIN_LOW = 128
 BIN_HIGH = NBINS // BIN_LOW
 F32 = jnp.float32
 BF16 = jnp.bfloat16
@@ -73,13 +76,81 @@
     return lax.dot_general(a, b, dims, preferred_element_type=F32, **kw)
 
 
+def sort_kernel(live_ref, vis_ref, tile_ref, u_ref, v_ref, index_ref, out_ref, *, peers):
+    channels, slots = vis_ref.shape[1:]
+    lane = lax.broadcasted_iota(jnp.int32, (8, slots), 1)
+    row = lax.broadcasted_iota(jnp.int32, (8, slots), 0)
+    slot = lax.broadcasted_iota(jnp.int32, (slots, slots), 0)
+    other = lax.broadcasted_iota(jnp.int32, (slots, slots), 1)
+    earlier = jnp.where(slot < other, 1.0, 0.0).astype(BF16)
+    for channel in range(channels):
+        own = slice(channel, channel + 1)
+        u_cell = jnp.minimum(tile_ref[own] * (G // peers) + u_ref[own], G - KW)
+        tile = jnp.where(lane[:1] < live_ref[own], u_cell // SUB, TILES)
+        member = jnp.where(row == tile, 1.0, 0.0)
+        before = dot(member.astype(BF16), earlier)
+        totals = jnp.sum(member, axis=1, keepdims=True)
+        start = jnp.zeros((1, 1), F32)
+        target = jnp.zeros((1, slots), F32)
+        for t in range(TILES):
+            target = jnp.where(tile == t, start + before[t : t + 1], target)
+            start = start + totals[t : t + 1]
+        target = jnp.where(tile == TILES, -1.0, target).astype(jnp.int32)
+        moved = jnp.where(slot == target, 1.0, 0.0).astype(BF16)
+        pieces = []
+        for part in range(2):
+            value = vis_ref[part, own]
+            for _ in range(3):
+                high = value.astype(BF16).astype(F32)
+                pieces.append(high)
+                value = value - high
+        v_cell = v_ref[own]
+        for cell in (u_cell, v_cell):
+            pieces.append((cell // V_LOW).astype(F32))
+            pieces.append((cell % V_LOW).astype(F32))
+        pieces.append(index_ref[0, own].astype(F32))
+        pieces.append(index_ref[1, own].astype(F32))
+        pieces.append(jnp.zeros((16 - len(pieces), slots), F32))
+        packed = dot(jnp.concatenate(pieces, axis=0).astype(BF16), moved, transposed=True)
+        real = packed[0:1] + packed[1:2] + packed[2:3]
+        imag = packed[3:4] + packed[4:5] + packed[5:6]
+        out_ref[channel] = jnp.concatenate(
+            [
+                real,
+                imag,
+                packed[6:7] * V_LOW + packed[7:8],
+                packed[8:9] * V_LOW + packed[9:10],
+                packed[10:12],
+                jnp.zeros((2, slots), F32),
+            ],
+            axis=0,
+        )
+        for t in range(TILES):
+            out_ref[channel, 6:7, t * (slots // TILES) : t * (slots // TILES) + 1] = totals[t : t + 1]
+
+
+def sorted_fields(peers, live_count, visibility, tile_of, u_within, v_cell, kernel_index):
+    channels, slots = visibility.shape[1:]
+    whole = pl.BlockSpec(memory_space=pltpu.VMEM)
+    return pl.pallas_call(
+        functools.partial(sort_kernel, peers=peers),
+        in_specs=[whole] * 6,
+        out_specs=whole,
+        out_shape=jax.ShapeDtypeStruct((channels, 8, slots), F32),
+        name="sort_by_tile",
+    )(live_count, visibility, tile_of[:, :, 0], u_within, v_cell, kernel_index)
+
+
 def image_kernel(
-    base_ref, live_ref, gathered_ref, kernel_ref, row_ref, coarse_ref, fine_ref, tap_ref,
-    out_ref, packed_ref, spectrum_ref, kernel_halves_ref, grid_ref, *, normalizer,
+    base_ref, live_ref, kernel_ref, row_ref, coarse_ref, fine_ref, tap_ref, *refs,
+    normalizer, peers,
 ):
+    field_refs = refs[:peers]
+    out_ref, packed_ref, spectrum_ref, kernel_halves_ref, grid_ref = refs[peers:]
+    owners, share_rows, width = out_ref.shape
+    me = base_ref[1]
     channel = pl.program_id(0)
-    peers, _, _, slots = gathered_ref.shape
-    width = out_ref.shape[1]
+    slots = field_refs[0].shape[2]
     table_rows = kernel_ref.shape[1]
 
     @pl.when(channel == 0)
@@ -91,26 +162,31 @@
         high = kernel_ref[...].astype(BF16).astype(F32)
         kernel_halves_ref[...] = jnp.concatenate([high, kernel_ref[...] - high], axis=0)
 
+    lane = lax.broadcasted_iota(jnp.int32, (8, slots + LANES), 1)
+    offsets = [jnp.int32(0)] * TILES
     packed_ref[...] = jnp.zeros_like(packed_ref)
-    offset = jnp.int32(0)
-    lane = lax.broadcasted_iota(jnp.int32, (8, slots + LANES), 1)
     for peer in range(peers):
-        live = live_ref[peer, channel]
-        block = offset // LANES
-        within = offset - block * LANES
         fields = jnp.concatenate(
-            [gathered_ref[peer, 0], jnp.zeros((8, LANES), F32)], axis=1
+            [field_refs[peer][0], jnp.zeros((8, LANES), F32)], axis=1
         )
-        fields = pltpu.roll(fields, within, 1)
-        kept = (lane >= within) & (lane < within + live)
-        window = pl.ds(pl.multiple_of(block * LANES, LANES), slots + LANES)
-        packed_ref[:, window] = packed_ref[:, window] + jnp.where(kept, fields, 0.0)
-        offset = offset + live
+        first = jnp.int32(0)
+        for tile in range(TILES):
+            count = live_ref[peer, channel, tile]
+            block = offsets[tile] // LANES
+            within = offsets[tile] - block * LANES
+            shift = within - first
+            width_all = slots + LANES
+            moved = pltpu.roll(fields, jnp.where(shift < 0, shift + width_all, shift), 1)
+            kept = (lane >= within) & (lane < within + count)
+            window = pl.ds(pl.multiple_of(block * LANES, LANES), width_all)
+            packed_ref[tile, :, window] = packed_ref[tile, :, window] + jnp.where(kept, moved, 0.0)
+            first = first + count
+            offsets[tile] = offsets[tile] + count
 
     grid_ref[...] = jnp.zeros_like(grid_ref)
 
-    def add_chunk(index, carry):
-        fields = packed_ref[:, pl.ds(pl.multiple_of(index * CHUNK, CHUNK), CHUNK)]
+    def add_chunk(tile, index, carry):
+        fields = packed_ref[tile, :, pl.ds(pl.multiple_of(index * CHUNK, CHUNK), CHUNK)]
         real, imag = fields[0:1], fields[1:2]
         cells = fields[2:6].astype(jnp.int32)
         u_cell, v_cell, index_u, index_v = cells[0:1], cells[1:2], cells[2:3], cells[3:4]
@@ -140,7 +216,8 @@
 
         chosen_u = jnp.where(table_row == index_u, 1.0, 0.0).astype(BF16)
         taps = dot(kernel_halves_ref[...].astype(BF16), chosen_u)
-        grid_row = lax.broadcasted_iota(jnp.int32, (SUB, CHUNK), 0)
+        grid_row = lax.broadcasted_iota(jnp.int32, (WINDOW, CHUNK), 0)
+        grid_row = grid_row + tile * (SUB // RADIX)
         rows = []
         for first in range(RADIX):
             tap = (first - u_cell) & (RADIX - 1)
@@ -161,14 +238,19 @@
                 )
                 halves.append(part.astype(BF16))
             rows.append(jnp.concatenate([halves[0], halves[0], halves[1]], axis=1))
-        grid_ref[...] += dot(jnp.concatenate(rows, axis=0), column, transposed=True)
+        tile_rows = dot(jnp.concatenate(rows, axis=0), column, transposed=True)
+        for first in range(RADIX):
+            start = first * BLOCK + tile * (SUB // RADIX)
+            grid_ref[start : start + WINDOW, :] += tile_rows[first * WINDOW : (first + 1) * WINDOW]
         return carry
 
-    lax.fori_loop(0, (offset + CHUNK - 1) // CHUNK, add_chunk, 0)
+    for tile in range(TILES):
+        chunks = (offsets[tile] + CHUNK - 1) // CHUNK
+        lax.fori_loop(0, chunks, functools.partial(add_chunk, tile), 0)
 
     parts = []
     for first in range(RADIX):
-        high, low = split(grid_ref[first * SUB : (first + 1) * SUB, :])
+        high, low = split(grid_ref[first * BLOCK : first * BLOCK + SUB, :])
         table = row_ref[first]
         table = jnp.concatenate([table[:, :SUB], table], axis=1)
         both = dot(table, jnp.concatenate([high, low, high], axis=0))
@@ -185,20 +267,25 @@
         (br - di, bi + dr),
     ]
     for block, (re, im) in enumerate(images):
-        window = slice(block * SUB, (block + 1) * SUB)
         power = (re * re + im * im) * normalizer
-
-        @pl.when(channel == 0)
-        def _():
-            out_ref[window, :] = power
-
-        @pl.when(channel != 0)
-        def _():
-            out_ref[window, :] += power
-
-
-def image_power(base_index, live, gathered, kernel, normalizer):
-    peers, channels, _, slots = gathered.shape
+        for row in range(0, SUB, share_rows):
+            owner = (block * SUB + row) // share_rows
+            turn = owner ^ me
+            place = (turn & 1) * (owners // 2) + turn // 2
+            part = power[row : row + share_rows]
+
+            @pl.when(channel == 0)
+            def _():
+                out_ref[place] = part
+
+            @pl.when(channel != 0)
+            def _():
+                out_ref[place] += part
+
+
+def image_power(place, owners, live, gathered, kernel, normalizer):
+    peers = len(gathered)
+    channels, _, slots = gathered[0].shape
     width = G // peers
     coarse, fine, taps = column_tables(peers)
     table_rows = kernel.shape[0]
@@ -209,34 +296,35 @@
         num_scalar_prefetch=2,
         grid=(channels,),
         in_specs=[
-            pl.BlockSpec((peers, 1, 8, slots), lambda c, *_: (0, c, 0, 0)),
             whole((KW, table_rows)),
             whole(rows.shape),
             own(coarse),
             own(fine),
             own(taps),
-        ],
-        out_specs=whole((G, width)),
+        ]
+        + [pl.BlockSpec((1, 8, slots), lambda c, *_: (c, 0, 0))] * peers,
+        out_specs=whole((owners, G // owners, width)),
         scratch_shapes=[
-            pltpu.VMEM((8, peers * slots + LANES), F32),
+            pltpu.VMEM((TILES, 8, peers * slots + LANES), F32),
             pltpu.VMEM((2 * width, 2 * table_rows), BF16),
             pltpu.VMEM((2 * KW, table_rows), F32),
-            pltpu.VMEM((G, 2 * width), F32),
+            pltpu.VMEM((RADIX * BLOCK, 2 * width), F32),
         ],
     )
     return pl.pallas_call(
-        functools.partial(image_kernel, normalizer=normalizer),
+        functools.partial(image_kernel, normalizer=normalizer, peers=peers),
         grid_spec=spec,
-        out_shape=jax.ShapeDtypeStruct((G, width), F32),
+        out_shape=jax.ShapeDtypeStruct((owners, G // owners, width), F32),
         compiler_params=pltpu.CompilerParams(dimension_semantics=("arbitrary",)),
         name="image_power",
-    )(base_index, live, gathered, kernel.T, rows, coarse, fine, taps)
-
-
-def bin_kernel(freq_ref, power_ref, bins_ref, share_ref, sums_ref, bins_t_ref):
-    share = power_ref[0]
-    for peer in range(1, power_ref.shape[0]):
-        share = share + power_ref[peer]
+    )(place, live, kernel.T, rows, coarse, fine, taps, *gathered)
+
+
+def bin_kernel(freq_ref, bins_ref, *refs):
+    share_ref, sums_ref, bins_t_ref = refs[-3:]
+    share = refs[0][...]
+    for ref in refs[1:-3]:
+        share = share + ref[...]
     share_ref[...] = share
     bins_t_ref[...] = bins_ref[...].astype(F32).T
     rows, width = share.shape
@@ -257,22 +345,25 @@
             one = slice(row, row + 1)
             at_high = high_row == bins[one] // BIN_LOW
             at_low = low_row == bins[one] % BIN_LOW
-            left.append(jnp.where(at_high, 1.0, 0.0).astype(BF16))
-            pieces = [jnp.where(at_low, x[one], 0.0) for x in (high, middle, low)]
-            pieces.append(jnp.where(at_low, 1.0, 0.0))
-            right.append(jnp.concatenate(pieces, axis=0).astype(BF16))
+            right.append(jnp.where(at_low, 1.0, 0.0).astype(BF16))
+            pieces = [jnp.where(at_high, x[one], 0.0) for x in (high, middle, low)]
+            pieces.append(jnp.where(at_high, 1.0, 0.0))
+            left.append(jnp.concatenate(pieces, axis=0).astype(BF16))
         if width % LANES == 0:
             left, right = [jnp.concatenate(left, axis=1)], [jnp.concatenate(right, axis=1)]
         for a, b in zip(left, right):
             running = running + dot(a, b, transposed=True)
         return running
 
-    zeros = jnp.zeros((BIN_HIGH, 4 * BIN_LOW), F32)
-    sums_ref[...] = lax.fori_loop(0, rows // group, add_group, zeros)
-
-
-def bin_power(freq_index, received, bin_map):
-    peers, rows, width = received.shape
+    zeros = jnp.zeros((4 * BIN_HIGH, BIN_LOW), F32)
+    sums = lax.fori_loop(0, rows // group, add_group, zeros, unroll=4)
+    pieces = [sums[i * BIN_HIGH : (i + 1) * BIN_HIGH] for i in range(4)]
+    sums = jnp.concatenate([pieces[0] + pieces[1] + pieces[2], pieces[3]], axis=0)
+    sums_ref[...] = jnp.broadcast_to(sums[None], sums_ref.shape)
+
+
+def bin_power(freq_index, received, bin_map, devices):
+    rows, width = received[0].shape
     if rows % LANES:
         bin_map = lax.dynamic_slice_in_dim(bin_map, freq_index[0] * rows, rows, 1)
         freq_index = jnp.zeros_like(freq_index)
@@ -280,12 +371,12 @@
         num_scalar_prefetch=1,
         grid=(1,),
         in_specs=[
-            pl.BlockSpec((peers, rows, width), lambda i, f: (0, 0, 0)),
             pl.BlockSpec((width, rows), lambda i, f: (0, f[0])),
-        ],
+        ]
+        + [pl.BlockSpec((rows, width), lambda i, f: (0, 0))] * len(received),
         out_specs=[
             pl.BlockSpec((rows, width), lambda i, f: (0, 0)),
-            pl.BlockSpec((BIN_HIGH, 4 * BIN_LOW), lambda i, f: (0, 0)),
+            pl.BlockSpec((devices, 2 * BIN_HIGH, BIN_LOW), lambda i, f: (0, 0, 0)),
         ],
         scratch_shapes=[pltpu.VMEM((rows, width), F32)],
     )
@@ -294,39 +385,47 @@
         grid_spec=spec,
         out_shape=[
             jax.ShapeDtypeStruct((rows, width), F32),
-            jax.ShapeDtypeStruct((BIN_HIGH, 4 * BIN_LOW), F32),
+            jax.ShapeDtypeStruct((devices, 2 * BIN_HIGH, BIN_LOW), F32),
         ],
         name="bin_power",
-    )(freq_index, received, bin_map)
-
-
-def sent_to_all(x, axis):
-    copies = jnp.broadcast_to(x[None], (lax.axis_size(axis),) + x.shape)
-    return lax.all_to_all(copies, axis, split_axis=0, concat_axis=0)
+    )(freq_index, bin_map, *received)
+
+
+def from_all(x, axis):
+    peers = lax.axis_size(axis)
+    turns = [[(i, (i + by) % peers) for i in range(peers)] for by in range(1, peers)]
+    return [x] + [lax.ppermute(x, axis, pairs) for pairs in turns]
+
+
+def shares_received(parts, axis):
+    owners = lax.axis_size(axis)
+    pairs = lambda turn: [(i, i ^ turn) for i in range(owners)]
+    half = owners // 2
+    other = lax.ppermute(parts[half:], axis, pairs(1))
+    sums = [parts[p] + other[p] for p in range(half)]
+    return [sums[0]] + [lax.ppermute(sums[p], axis, pairs(2 * p)) for p in range(1, half)]
 
 
 def per_device(visibility, tile_of, u_within, v_cell, kernel_index, kernel, live_count, bin_map):
     base_count = lax.axis_size("base")
     freq_count = lax.axis_size("freq")
-    tile_rows = G // base_count
     channels_here, slots = visibility.shape[1:]
-    u_cell = jnp.minimum(tile_of[:, :, 0] * tile_rows + u_within, G - KW)
-    cells = jnp.stack([u_cell, v_cell, kernel_index[0], kernel_index[1]]).astype(F32)
-    counts = jnp.broadcast_to(live_count.astype(F32)[None], (1, channels_here, slots))
-    fields = jnp.concatenate([visibility, cells, counts, jnp.zeros_like(counts)], axis=0)
-    gathered = sent_to_all(fields.transpose(1, 0, 2), "base")
-    live = gathered[:, :, 6, 0].astype(jnp.int32)
+    fields = sorted_fields(
+        base_count, live_count, visibility, tile_of, u_within, v_cell, kernel_index
+    )
+    gathered = from_all(fields, "base")
+    step = slots // TILES
+    live = jnp.stack([fields[:, 6, ::step] for fields in gathered]).astype(jnp.int32)
     normalizer = 1.0 / (channels_here * freq_count * slots * base_count)
-    power_part = image_power(
-        lax.axis_index("base")[None], live, gathered, kernel, normalizer
-    )
-    blocks = power_part.reshape(freq_count, G // freq_count, -1)
-    received = lax.all_to_all(blocks, "freq", split_axis=0, concat_axis=0)
-    power_share, sums = bin_power(lax.axis_index("freq")[None], received, bin_map)
-    sums = sums.reshape(BIN_HIGH, 4, BIN_LOW)
-    sums = jnp.stack([sums[:, 0] + sums[:, 1] + sums[:, 2], sums[:, 3]]).reshape(2 * NBINS)
-    sums = jnp.sum(sent_to_all(sums, ("freq", "base")), axis=0)
-    return power_share, sums[:NBINS] / sums[NBINS:]
+    place = jnp.stack([lax.axis_index("base"), lax.axis_index("freq")])
+    power_part = image_power(place, freq_count, live, gathered, kernel, normalizer)
+    received = shares_received(power_part, "freq")
+    power_share, sums = bin_power(
+        lax.axis_index("freq")[None], received, bin_map, freq_count * base_count
+    )
+    sums = lax.all_to_all(sums, ("freq", "base"), split_axis=0, concat_axis=0)
+    sums = jnp.sum(sums, axis=0)
+    return power_share, (sums[:BIN_HIGH] / sums[BIN_HIGH:]).reshape(NBINS)
 
 
 def solution(mesh):

time: 81 us -> 69.1 us (0.85)
  waiting for transfers between devices: 21.5 us -> 11.5 us
  Pallas kernels: 31 us -> 25 us
  local copies, waits for them, and re-layouts: 3.58 us -> 5.42 us
  starting transfers between devices: 10.1 us -> 11 us
    all_to_all x2 -> x0, waiting for transfers between devices: 21.5 us -> none  [the longest x1 15.4 us: per_device(): received = lax.all_to_all(blocks, 'freq', split_axis=0, concat_axis=0)]
    ppermute x0 -> x7, waiting for transfers between devices: none -> 11.5 us  [the longest x3 6.32 us: shares_received(): lax.ppermute(sums[p], axis, pairs(2 * p))]
    ppermute x0 -> x7, starting transfers between devices: none -> 11 us  [the longest x3 6.09 us: from_all(): return [x] + [lax.ppermute(x, axis, pairs) for pairs in turns]]
    all_to_all x2 -> x0, starting transfers between devices: 10.1 us -> none  [the longest x1 6.35 us: sent_to_all(): return lax.all_to_all(copies, axis, split_axis=0, concat_axis=0)]
    pallas_call x1 -> x2, Pallas kernels: 25.5 us -> 20.3 us  [the longest x1 18.2 us: image_power(): pl.pallas_call(functools.partial(image_kernel, normalizer=normalizer, pee...]
    unnamed x4 -> x14, local copies, waits for them, and re-layouts: 0.98 us -> 3.23 us
    slice x0 -> x5, local copies, waits for them, and re-layouts: none -> 2.19 us  [the longest x4 1.11 us: per_device(): fields[:, 6, ::step]]
    add x1, other arithmetic: 0.01 us -> 1.81 us  [shares_received(): sums = [parts[p] + other[p] for p in range(half)]]
  transfers between devices with their start and end apart: 2 -> 7, of which waited for: 2 -> 6; matrix products, arithmetic and copies ran while one was open for 0% -> 2% of each run, Pallas kernels for 0% -> 0%
where the time goes in v2:
time: 69.1 us; the launch traced here: 68.1 us
  Pallas kernels  25 us (36%)
  waiting for transfers between devices  11.5 us (17%)
  starting transfers between devices  11 us (16%)
  blocking collectives  10.9 us (16%)
  local copies, waits for them, and re-layouts  5.42 us (8%)
  other arithmetic  3.65 us (5%)
    pallas_call x1, Pallas kernels, image_power(): pl.pallas_call(functools.partial(image_kernel, normalizer=normalizer, pee...  18.2 us
    all_to_all x1, blocking collectives, per_device(): sums = lax.all_to_all(sums, ('freq', 'base'), split_axis=0, concat_axis=0)  10.9 us
    ppermute x3, waiting for transfers between devices, shares_received(): lax.ppermute(sums[p], axis, pairs(2 * p))  6.32 us
    ppermute x3, starting transfers between devices, from_all(): return [x] + [lax.ppermute(x, axis, pairs) for pairs in turns]  6.09 us
    ppermute x3, starting transfers between devices, shares_received(): lax.ppermute(sums[p], axis, pairs(2 * p))  4.85 us
    pallas_call x1, Pallas kernels, bin_power(): pl.pallas_call(bin_kernel, grid_spec=spec, out_shape=[jax.ShapeDtypeStruc...  4.64 us
    ppermute x3, waiting for transfers between devices, from_all(): return [x] + [lax.ppermute(x, axis, pairs) for pairs in turns]  3.27 us
    unnamed x14, local copies, waits for them, and re-layouts  3.23 us
  transfers between devices with their start and end apart: 7, of which 6 were waited for; matrix products, arithmetic and copies ran while one was open for 2% of the time, Pallas kernels for 0%

profile of v2, /device:TPU:0, one launch (start us, length us, event | category | flops | bytes accessed | tf_op | source)
XLA Modules:
  0.0 68.1 jit_solution(8663902256523155102)
XLA Ops:
  0.6 1.3 %copy.14.live_ref = s32[2,1]{1,0:T(2,128)} copy(s32[2,1]{0,1:T(1,128)} %param.18) | data formatting | bytes 16 | tf_op args[6]
  1.9 1.3 %copy.17 = s32[2,512,1]{1,0,2:T(2,128)} copy(s32[2,512,1]{1,2,0:T(1,128)} %param.13) | data formatting | bytes 8192
  3.2 2.2 %sort_by_tile.1.refs_0_ = f32[2,8,512]{2,1,0:T(8,128)} custom-call(s32[2,1]{1,0:T(2,128)} %copy.14.live_ref, f32[2,2,512]{2,1,0:T(2,128)} %vis_ref.1, s32[2,512]{1,0:T(2,128)} %bitcast.20, s32[2,512]{1,0:T(2,128)} %u_ref.1, s32[2,512]{1,0:T(2,128)} %v_ref.1, s32[2,2,512]{2,1,0:T(2,128)} %index_ref.1), custom_call_target="tpu_custom_call" | custom-call | tf_op jit(solution)/shard_map/sort_by_tile/pallas_call | solution.py:135
  5.4 5.1 %collective-permute-start.2 = (f32[2,8,512]{2,1,0:T(8,128)}, f32[2,8,512]{2,1,0:T(8,128)S(1)}, u32[]{:S(2)}, u32[]{:S(2)}) collective-permute-start(f32[2,8,512]{2,1,0:T(8,128)} %sort_by_tile.1.refs_0_), channel_id=1, source_target_pairs={{0,3},{1,0},{2,1},{3,2},{4,7},{5,4},{6,5},{7,6},{8,11},{9,8},{10,9... | collective-permute-start | bytes 98312 | tf_op jit(solution)/shard_map/ppermute | solution.py:397
  10.5 0.0 collective-permute-start.1
  10.5 1.0 %collective-permute-start = (f32[2,8,512]{2,1,0:T(8,128)}, f32[2,8,512]{2,1,0:T(8,128)S(1)}, u32[]{:S(2)}, u32[]{:S(2)}) collective-permute-start(f32[2,8,512]{2,1,0:T(8,128)} %sort_by_tile.1.refs_0_), channel_id=1, source_target_pairs={{0,1},{1,2},{2,3},{3,0},{4,5},{5,6},{6,7},{7,4},{8,9},{9,10},{10,1... | collective-permute-start | bytes 98312 | tf_op jit(solution)/shard_map/ppermute | solution.py:397
  11.5 0.6 pad_add_fusion.base_ref
  12.1 0.8 %slice.45 = f32[2,1,4]{2,1,0:T(1,128)S(1)} slice(f32[2,8,512]{2,1,0:T(8,128)} %sort_by_tile.1.refs_0_), slice={[0:2:1], [6:7:1], [0:512:128]} | slice | bytes 64 | tf_op jit(solution)/shard_map/slice | solution.py:418
  12.9 0.0 collective-permute-done.2.refs_3_
  12.9 0.0 copy-start.3
  12.9 0.1 slice.48
  13.0 2.5 %collective-permute-done.1.refs_2_ = f32[2,8,512]{2,1,0:T(8,128)S(1)} collective-permute-done((f32[2,8,512]{2,1,0:T(8,128)}, f32[2,8,512]{2,1,0:T(8,128)S(1)}, u32[]{:S(2)}, u32[]{:S(2)}) %collective-permute-start.1) | collective-permute-done | bytes 32800 | tf_op jit(solution)/shard_map/ppermute | solution.py:397
  15.5 0.0 copy-start.4
  15.5 0.1 slice.47
  15.6 0.8 %collective-permute-done.refs_1_ = f32[2,8,512]{2,1,0:T(8,128)S(1)} collective-permute-done((f32[2,8,512]{2,1,0:T(8,128)}, f32[2,8,512]{2,1,0:T(8,128)S(1)}, u32[]{:S(2)}, u32[]{:S(2)}) %collective-permute-start) | collective-permute-done | bytes 32800 | tf_op jit(solution)/shard_map/ppermute | solution.py:397
  16.4 0.0 copy-start.5
  16.4 0.1 slice.46
  16.5 0.6 maximum_convert_fusion.live_ref
  17.1 0.0 copy-done.3
  17.1 0.0 copy-done.4
  17.1 0.0 copy-done.5
  17.1 18.2 %image_power.1 = f32[8,128,256]{2,1,0:T(8,128)} custom-call(s32[2]{0:T(128)} %pad_add_fusion.base_ref, s32[4,2,4]{2,1,0:T(2,128)} %maximum_convert_fusion.live_ref, f32[8,128]{1,0:T(8,128)} %bitcast.21, bf16[4,512,512]{2,1,0:T(8,128)(2,1)} %constant.19.clone.row_ref, bf16[4,512,192]{2,1,0:T(8,128)(2,1)} %constant.20.clone.coarse_ref, ...), custom_call_target="tpu_custom_call" | custom-call | tf_op jit(solution)/shard_map/image_power/pallas_call | solution.py:314
  35.2 1.1 %slice.61 = f32[4,128,256]{2,1,0:T(8,128)S(1)} slice(f32[8,128,256]{2,1,0:T(8,128)} %image_power.1), slice={[4:8], [0:128], [0:256]} | slice | bytes 1048576 | tf_op jit(solution)/shard_map/slice | solution.py:404
  36.3 0.1 collective-permute-start.3
  36.4 1.9 %collective-permute-done.3 = f32[4,128,256]{2,1,0:T(8,128)S(1)} collective-permute-done((f32[4,128,256]{2,1,0:T(8,128)S(1)}, f32[4,128,256]{2,1,0:T(8,128)S(1)}, u32[]{:S(2)}, u32[]{:S(2)}) %collective-permute-start.3) | collective-permute-done | bytes 524320 | tf_op jit(solution)/shard_map/ppermute | solution.py:404
  38.3 1.8 %fusion = (f32[128,256]{1,0:T(8,128)S(1)}, f32[128,256]{1,0:T(8,128)S(1)}, f32[128,256]{1,0:T(8,128)S(1)}, f32[128,256]{1,0:T(8,128)}) fusion(f32[4,128,256]{2,1,0:T(8,128)S(1)} %collective-permute-done.3, f32[8,128,256]{2,1,0:T(8,128)} %image_power.1), kind=kLoop, calls=%fused_computation.1 | loop fusion | flops 131072 | bytes 1572864 | tf_op jit(solution)/shard_map/add | solution.py:405
  40.1 4.3 %collective-permute-start.6 = (f32[128,256]{1,0:T(8,128)S(1)}, f32[128,256]{1,0:T(8,128)S(1)}, u32[]{:S(2)}, u32[]{:S(2)}) collective-permute-start(f32[128,256]{1,0:T(8,128)S(1)} %get-tuple-element.6), channel_id=1, source_target_pairs={{0,24},{4,28},{8,16},{12,20},{16,8},{20,12},{24,0},{28,4},{1,25},{... | collective-permute-start | bytes 393224 | tf_op jit(solution)/shard_map/ppermute | solution.py:406
  44.4 0.0 collective-permute-start.5
  44.4 0.6 collective-permute-start.4
  45.0 3.4 %collective-permute-done.6.refs_3_ = f32[128,256]{1,0:T(8,128)S(1)} collective-permute-done((f32[128,256]{1,0:T(8,128)S(1)}, f32[128,256]{1,0:T(8,128)S(1)}, u32[]{:S(2)}, u32[]{:S(2)}) %collective-permute-start.6) | collective-permute-done | bytes 131104 | tf_op jit(solution)/shard_map/ppermute | solution.py:406
  48.4 0.0 copy-start
  48.4 2.6 %collective-permute-done.5.refs_2_ = f32[128,256]{1,0:T(8,128)S(1)} collective-permute-done((f32[128,256]{1,0:T(8,128)S(1)}, f32[128,256]{1,0:T(8,128)S(1)}, u32[]{:S(2)}, u32[]{:S(2)}) %collective-permute-start.5) | collective-permute-done | bytes 131104 | tf_op jit(solution)/shard_map/ppermute | solution.py:406
  51.0 0.0 copy-start.1
  51.0 0.3 collective-permute-done.4.refs_1_
  51.3 0.0 copy-start.2
  51.3 0.0 copy-done
  51.3 0.4 copy-done.1
  51.6 0.3 copy-done.2
  51.9 4.6 %bin_power.1 = (f32[128,256]{1,0:T(8,128)}, f32[32,8,128]{2,1,0:T(8,128)}) custom-call(s32[1]{0:T(128)} %bitcast.freq_ref, s32[256,1024]{1,0:T(8,128)} %bins_ref.1, f32[128,256]{1,0:T(8,128)} %get-tuple-element.9.refs_0_, f32[128,256]{1,0:T(8,128)} %copy-done.2, f32[128,256]{1,0:T(8,128)} %copy-done.1, f32[128,256]{1,0:T(8,128)} %copy-done), custom_call_target="tpu_custom_call" | custom-call | tf_op jit(solution)/shard_map/bin_power/pallas_call | solution.py:383
  56.6 10.9 %all_to_all.5 = f32[32,8,128]{2,1,0:T(8,128)S(1)} all-to-all(f32[32,8,128]{2,1,0:T(8,128)} %get-tuple-element.5), channel_id=1, replica_groups=mesh['freq'=8,'base'=4] {'freq','base'}, dimensions={0} | all-to-all | bytes 262144 | tf_op jit(solution)/shard_map/all_to_all | solution.py:426
  67.6 0.6 fusion.4
  (1 shorter events, 0.0 us)
Async XLA Ops:
  5.4 7.5 %collective-permute-start.2 = (f32[2,8,512]{2,1,0:T(8,128)}, f32[2,8,512]{2,1,0:T(8,128)S(1)}, u32[]{:S(2)}, u32[]{:S(2)}) collective-permute-start(f32[2,8,512]{2,1,0:T(8,128)} %sort_by_tile.1.refs_0_), channel_id=1, source_target_pairs={{0,3},{1,0},{2,1},{3,2},{4,7},{5,4},{6,5},{7,6},{8,11},{9,8},{10,9... | collective-permute-start | bytes 98312 | tf_op jit(solution)/shard_map/ppermute | solution.py:397
  10.5 5.0 %collective-permute-start.1 = (f32[2,8,512]{2,1,0:T(8,128)}, f32[2,8,512]{2,1,0:T(8,128)S(1)}, u32[]{:S(2)}, u32[]{:S(2)}) collective-permute-start(f32[2,8,512]{2,1,0:T(8,128)} %sort_by_tile.1.refs_0_), channel_id=1, source_target_pairs={{0,2},{1,3},{2,0},{3,1},{4,6},{5,7},{6,4},{7,5},{8,10},{9,11},{10,... | collective-permute-start | bytes 98312 | tf_op jit(solution)/shard_map/ppermute | solution.py:397
  10.5 5.9 %collective-permute-start = (f32[2,8,512]{2,1,0:T(8,128)}, f32[2,8,512]{2,1,0:T(8,128)S(1)}, u32[]{:S(2)}, u32[]{:S(2)}) collective-permute-start(f32[2,8,512]{2,1,0:T(8,128)} %sort_by_tile.1.refs_0_), channel_id=1, source_target_pairs={{0,1},{1,2},{2,3},{3,0},{4,5},{5,6},{6,7},{7,4},{8,9},{9,10},{10,1... | collective-permute-start | bytes 98312 | tf_op jit(solution)/shard_map/ppermute | solution.py:397
  12.9 4.2 %copy-start.3 = (f32[2,8,512]{2,1,0:T(8,128)}, f32[2,8,512]{2,1,0:T(8,128)S(1)}, u32[]{:S(2)}) copy-start(f32[2,8,512]{2,1,0:T(8,128)S(1)} %collective-permute-done.2.refs_3_) | copy-start | bytes 98308
  15.5 1.6 %copy-start.4 = (f32[2,8,512]{2,1,0:T(8,128)}, f32[2,8,512]{2,1,0:T(8,128)S(1)}, u32[]{:S(2)}) copy-start(f32[2,8,512]{2,1,0:T(8,128)S(1)} %collective-permute-done.1.refs_2_) | copy-start | bytes 98308
  16.4 0.7 %copy-start.5 = (f32[2,8,512]{2,1,0:T(8,128)}, f32[2,8,512]{2,1,0:T(8,128)S(1)}, u32[]{:S(2)}) copy-start(f32[2,8,512]{2,1,0:T(8,128)S(1)} %collective-permute-done.refs_1_) | copy-start | bytes 98308
  36.3 2.0 %collective-permute-start.3 = (f32[4,128,256]{2,1,0:T(8,128)S(1)}, f32[4,128,256]{2,1,0:T(8,128)S(1)}, u32[]{:S(2)}, u32[]{:S(2)}) collective-permute-start(f32[4,128,256]{2,1,0:T(8,128)S(1)} %slice.61), channel_id=1, source_target_pairs={{0,4},{4,0},{8,12},{12,8},{16,20},{20,16},{24,28},{28,24},{1,5},{5... | collective-permute-start | bytes 1572872 | tf_op jit(solution)/shard_map/ppermute | solution.py:404
  40.1 8.2 %collective-permute-start.6 = (f32[128,256]{1,0:T(8,128)S(1)}, f32[128,256]{1,0:T(8,128)S(1)}, u32[]{:S(2)}, u32[]{:S(2)}) collective-permute-start(f32[128,256]{1,0:T(8,128)S(1)} %get-tuple-element.6), channel_id=1, source_target_pairs={{0,24},{4,28},{8,16},{12,20},{16,8},{20,12},{24,0},{28,4},{1,25},{... | collective-permute-start | bytes 393224 | tf_op jit(solution)/shard_map/ppermute | solution.py:406
  44.4 6.6 %collective-permute-start.5 = (f32[128,256]{1,0:T(8,128)S(1)}, f32[128,256]{1,0:T(8,128)S(1)}, u32[]{:S(2)}, u32[]{:S(2)}) collective-permute-start(f32[128,256]{1,0:T(8,128)S(1)} %get-tuple-element.7), channel_id=1, source_target_pairs={{0,16},{4,20},{8,24},{12,28},{16,0},{20,4},{24,8},{28,12},{1,17},{... | collective-permute-start | bytes 393224 | tf_op jit(solution)/shard_map/ppermute | solution.py:406
  44.4 6.9 %collective-permute-start.4 = (f32[128,256]{1,0:T(8,128)S(1)}, f32[128,256]{1,0:T(8,128)S(1)}, u32[]{:S(2)}, u32[]{:S(2)}) collective-permute-start(f32[128,256]{1,0:T(8,128)S(1)} %get-tuple-element.8), channel_id=1, source_target_pairs={{0,8},{4,12},{8,0},{12,4},{16,24},{20,28},{24,16},{28,20},{1,9},{5... | collective-permute-start | bytes 393224 | tf_op jit(solution)/shard_map/ppermute | solution.py:406
  48.4 2.9 %copy-start = (f32[128,256]{1,0:T(8,128)}, f32[128,256]{1,0:T(8,128)S(1)}, u32[]{:S(2)}) copy-start(f32[128,256]{1,0:T(8,128)S(1)} %collective-permute-done.6.refs_3_) | copy-start | bytes 393220
  51.0 0.6 copy-start.1
  51.3 0.7 copy-start.2
